TPU v7x, 256 devices: a 4x2x16 block of a 4x16x16 slice. The times are simulated.
256 devices in a mesh: groups: 2 (over y), seq: 32 (over z, core), role: 4 (over x).
Axes of the slice: x: 4, y: 2, z: 16, core: 2. Of those that a mesh axis runs over, the one named last changes fastest.
The devices are a block of a 4x16x16 slice.
Arguments:
- queries: bfloat16 [8, 4096, 4096], P(('groups', 'role'), 'seq'), parts along dimension 0, may hold values from -500 to 500
- keys: bfloat16 [8, 4096, 4096], P(('groups', 'role'), 'seq'), parts along dimension 0, may hold values from -500 to 500
- values: bfloat16 [8, 4096, 4096], P(('groups', 'role'), 'seq'), parts along dimension 0, may hold values from -6 to 6
- q_gain: float32 [4096], replicated, may hold values from 1.2 to 1.8
- k_gain: float32 [4096], replicated, may hold values from 1.2 to 1.8
- latent_frames: bfloat16 [8, 64, 160, 384], P(('groups', 'role'), 'seq'), parts along dimension 0, may hold values from -6 to 6
- frame_cache: bfloat16 [4, 64, 160, 384], P('groups', 'seq'), parts along dimension 0, may hold values from -6 to 6
- vae_gain: float32 [384], replicated, may hold values from 0.5 to 1.5
- conv_weight: bfloat16 [3, 3, 3, 384, 384], replicated, may hold values from -0.0625 to 0.0625
- conv_bias: float32 [384], replicated, may hold values from -1.5 to 1.5
Outputs:
- attended: bfloat16 [8, 4096, 4096], P(('groups', 'role'), 'seq'), parts along dimension 0
- decoded: bfloat16 [8, 64, 160, 384], P(('groups', 'role'), 'seq'), parts along dimension 0
There are 2 independent parts, one for each index of `groups`. A program takes and returns all parts, laid end to end along the dimension named above; an argument that names none is the same for every part. Nothing has to cross between parts.
All inputs are finite; a program needn't handle non-finite values.
Results may differ from a plain program's by a relative error of at most 0.0025.
The roundings to bfloat16 on the way count: a program that leaves them out, or rounds other values in their place, can miss the bound.
Values may be sent and summed in bfloat16 or wider, within the bound.
A program may use at most 128 MiB of HBM per device.

v0:
```python
import jax
import jax.numpy as jnp
from jax import lax
from jax.sharding import Mesh
from jax.sharding import PartitionSpec as P

HEAD_DIM = 128
SEQ = ("seq_0", "seq_1")


EPSILON = 1e-06


def from_behind(value, axis, steps):
    count = lax.axis_size(axis)
    leading, last = (max(0, -steps), min(count, count - steps))
    return lax.ppermute(value, axis, [(source, source + steps) for source in range(leading, last)])


def extended(block, sides, width):
    for axis, dim in sides:
        count = lax.axis_size(axis)
        forward = [(i, i + 1) for i in range(count - 1)]
        backward = [(target, source) for source, target in forward]
        low = lax.ppermute(
            lax.slice_in_dim(block, block.shape[dim] - width, None, axis=dim), axis, forward
        )
        high = lax.ppermute(lax.slice_in_dim(block, 0, width, axis=dim), axis, backward)
        block = jnp.concatenate([low, block, high], axis=dim)
    return block


def sent_together(arrays, axis, split_dim, concat_dim, along):
    ends, at = ([], 0)
    for a in arrays[:-1]:
        at += a.shape[along]
        ends.append(at)
    both = jnp.concatenate(arrays, axis=along)
    return tuple(
        jnp.split(
            lax.all_to_all(both, axis, split_axis=split_dim, concat_axis=concat_dim, tiled=True),
            ends,
            axis=along,
        )
    )


def split_up(value, dim, size):
    lengths = value.shape
    blocks = value.reshape(*lengths[:dim], size, lengths[dim] // size, *lengths[dim + 1 :])
    return jnp.moveaxis(blocks, dim, 0)


def in_order(blocks, dim):
    lengths = list(blocks.shape[1:])
    lengths[dim] *= blocks.shape[0]
    return jnp.moveaxis(blocks, 0, dim).reshape(lengths)


def exchange_in_order(blocks, axes, order):
    inside = blocks.shape[1:]
    whole = blocks.reshape(*(lax.axis_size(a) for a in axes), *inside)
    for k in order:
        whole = lax.all_to_all(whole, axes[k], k, k, tiled=True)
    return whole.reshape(-1, *inside)


def two_step_exchange(value, groups, order, split_dim, concat_dim):
    size = lax.axis_size(groups[0]) * lax.axis_size(groups[1])
    blocks = split_up(value, split_dim, size)
    return in_order(exchange_in_order(blocks, groups, order), concat_dim)


def rms_scale(rows, gain):
    values_f = rows.astype(jnp.float32)
    mean_sq = jnp.mean(values_f * values_f, axis=-1, keepdims=True)
    return values_f * lax.rsqrt(mean_sq + EPSILON) * gain


def attend(parts):
    queries, keys, values = parts
    length = queries.shape[1]
    block = min(512, length)
    scale = queries.shape[4] ** (-0.5)
    by_head = (
        jnp.moveaxis(queries[0, :, 0], 1, 0),
        jnp.moveaxis(keys[0, :, 0], 1, 0),
        jnp.moveaxis(values[0, :, 0], 1, 0),
    )

    def one_head(triple):
        q_head, k_head, v_head = triple

        def one_block(start):
            rows = lax.dynamic_slice_in_dim(q_head, start, block, 0)
            scores = (
                jnp.einsum("qd,kd->qk", rows, k_head, preferred_element_type=jnp.float32) * scale
            )
            top = jnp.max(scores, axis=1, keepdims=True)
            weights = jnp.exp(scores - top)
            total = jnp.sum(weights, axis=1, keepdims=True)
            mixed = (
                jnp.dot(weights.astype(jnp.bfloat16), v_head, preferred_element_type=jnp.float32)
                / total
            )
            return mixed.astype(jnp.bfloat16)

        starts = jnp.arange(length // block, dtype=jnp.int32) * block
        return lax.map(one_block, starts).reshape(length, -1)

    result = lax.map(one_head, by_head)
    return jnp.moveaxis(result, 0, 1)[None, :, None]


def history(own, past, place):
    before = from_behind(own, "role", 1)
    earlier = from_behind(own, "role", 2)
    one_back = jnp.where(place >= 1, before, past[1:2])
    two_back = jnp.where(place >= 2, earlier, jnp.where(place >= 1, past[1:2], past[0:1]))
    return jnp.concatenate([two_back, one_back, own], axis=0)


def body(
    queries,
    keys,
    values,
    q_gain,
    k_gain,
    latent_frames,
    frame_cache,
    vae_gain,
    conv_weight,
    conv_bias,
):
    tok_local = queries.shape[1]
    width = queries.shape[2]
    depth = HEAD_DIM
    heads = width // depth
    groups_seq = lax.axis_size(SEQ)
    per_group = heads // groups_seq
    layout = (1, tok_local, groups_seq, per_group, depth)
    q_normed = rms_scale(queries, q_gain).astype(jnp.bfloat16).reshape(layout)
    k_normed = rms_scale(keys, k_gain).astype(jnp.bfloat16).reshape(layout)
    v_split = values.reshape(layout)
    activated_own = jax.nn.silu(rms_scale(latent_frames, vae_gain)).astype(jnp.bfloat16)
    activated_past = jax.nn.silu(rms_scale(frame_cache, vae_gain)).astype(jnp.bfloat16)
    place = lax.axis_index("role")
    stacked = history(activated_own, activated_past, place)
    stacked = extended(stacked, ((SEQ, 1),), 1)
    stacked = jnp.pad(stacked, ((0, 0), (0, 0), (1, 1), (0, 0)))
    rows = latent_frames.shape[1]
    cols = latent_frames.shape[2]
    chans = latent_frames.shape[3]
    pieces = []
    for a in range(3):
        for b in range(3):
            for e in range(3):
                pieces.append(stacked[a, b : b + rows, e : e + cols, :])
    columns = jnp.concatenate(pieces, axis=-1).reshape(rows * cols, 27 * chans)
    weight = conv_weight.reshape(27 * chans, chans)
    conv = jnp.dot(columns, weight, preferred_element_type=jnp.float32).reshape(
        1, rows, cols, chans
    )
    decoded = (latent_frames.astype(jnp.float32) + conv + conv_bias).astype(jnp.bfloat16)
    moved = sent_together((q_normed, k_normed, v_split), SEQ, 2, 1, 0)
    mixed = attend(moved)
    returned = two_step_exchange(mixed, ("seq_0", "seq_1"), (1, 0), 1, 2)
    attended = returned.reshape(1, tok_local, width)
    return (attended, decoded)


def solution(mesh):
    finer = Mesh(
        mesh.devices.reshape(mesh.shape["groups"], 16, 2, mesh.shape["role"]),
        ("groups", "seq_0", "seq_1", "role"),
    )
    in_specs = (
        P(("groups", "role"), SEQ, None),
        P(("groups", "role"), SEQ, None),
        P(("groups", "role"), SEQ, None),
        P(),
        P(),
        P(("groups", "role"), SEQ, None, None),
        P("groups", SEQ, None, None),
        P(),
        P(),
        P(),
    )
    out_specs = (P(("groups", "role"), SEQ, None), P(("groups", "role"), SEQ, None, None))
    return jax.shard_map(body, mesh=finer, in_specs=in_specs, out_specs=out_specs, check_vma=False)
```

profile of v0, /device:TPU:33, one launch (start us, length us, event | category | flops | bytes accessed | tf_op | source)
XLA Modules:
  0.0 325.9 jit_solution(3483607385380315178)
XLA Ops:
  9.5 2.8 copy.21
  12.3 25.6 %all-to-all-start = ((bf16[3,128,32,1,128]{4,1,0,3,2:T(8,128)(2,1)}), bf16[3,128,32,1,128]{4,1,0,3,2:T(8,128)(2,1)}, u32[]{:S(2)}, u32[]{:S(2)}) async-start(bf16[3,128,32,1,128]{4,1,0,3,2:T(8,128)(2,1)} %copy.21), calls=%async_computation | async-start | bytes 6291456 | tf_op jit(solution)/shard_map/all_to_all | solution.py:41
  38.3 5.0 %collective-permute-start = (bf16[1,2,160,384]{3,2,1,0:T(8,128)(2,1)S(1)}, bf16[1,2,160,384]{3,2,1,0:T(8,128)(2,1)S(1)}, u32[]{:S(2)}, u32[]{:S(2)}) collective-permute-start(bf16[1,2,160,384]{3,2,1,0:T(8,128)(2,1)S(1)} %fusion.61), channel_id=1, source_target_pairs={{0,2},{1,3},{4,6},{5,7},{8,10},{9,11},{12,14},{13,15},{16,18},{17,... | collective-permute-start | bytes 737288 | tf_op jit(solution)/shard_map/ppermute | solution.py:17
  43.3 2.4 collective-permute-start.1
  47.9 5.3 %collective-permute-done.1 = bf16[1,2,160,384]{3,2,1,0:T(8,128)(2,1)S(1)} collective-permute-done((bf16[1,2,160,384]{3,2,1,0:T(8,128)(2,1)S(1)}, bf16[1,2,160,384]{3,2,1,0:T(8,128)(2,1)S(1)}, u32[]{:S(2)}, u32[]{:S(2)}) %collective-permute-start.1) | collective-permute-done | bytes 245792 | tf_op jit(solution)/shard_map/ppermute | solution.py:17
  53.4 4.7 %collective-permute-start.2 = (bf16[3,1,160,384]{3,2,1,0:T(8,128)(2,1)S(1)}, bf16[3,1,160,384]{3,2,1,0:T(8,128)(2,1)S(1)}, u32[]{:S(2)}, u32[]{:S(2)}) collective-permute-start(bf16[3,1,160,384]{3,2,1,0:T(8,128)(2,1)S(1)} %get-tuple-element.67), channel_id=1, source_target_pairs={{0,4},{4,8},{8,12},{12,16},{16,20},{20,24},{24,28},{28,32},{32,36}... | collective-permute-start | bytes 1105928 | tf_op jit(solution)/shard_map/ppermute | solution.py:25
  60.2 116.5 %collective-permute-done.2 = bf16[3,1,160,384]{3,2,1,0:T(8,128)(2,1)S(1)} collective-permute-done((bf16[3,1,160,384]{3,2,1,0:T(8,128)(2,1)S(1)}, bf16[3,1,160,384]{3,2,1,0:T(8,128)(2,1)S(1)}, u32[]{:S(2)}, u32[]{:S(2)}) %collective-permute-start.2) | collective-permute-done | bytes 368672 | tf_op jit(solution)/shard_map/ppermute | solution.py:25
  176.7 2.5 collective-permute-done.3
  188.8 3.5 %fusion.65 = (bf16[1,32,128,1,1,128]{5,2,0,1,4,3:T(8,128)(2,1)}, bf16[1,32,128,1,1,128]{5,2,0,1,4,3:T(8,128)(2,1)S(1)}, bf16[1,32,128,1,1,128]{5,2,0,1,4,3:T(8,128)(2,1)}) fusion(bf16[3,32,128,1,1,128]{5,2,0,1,4,3:T(8,128)(2,1)} %bitcast.6), kind=kLoop, calls=%fused_computation.102 | loop fusion | bytes 6291456 | tf_op jit(solution)/shard_map/split | solution.py:40
  192.3 67.2 %while.17 = (s32[]{:T(128)}, bf16[8,512,128]{2,1,0:T(8,128)(2,1)}, s32[8]{0:T(128)S(1)}, bf16[4096,128]{1,0:T(8,128)(2,1)}, bf16[4096,128]{1,0:T(8,128)(2,1)S(1)...) while((s32[]{:T(128)}, bf16[8,512,128]{2,1,0:T(8,128)(2,1)}, s32[8]{0:T(128)S(1)}, ...), condition=%wide.region_5.6_spmd, body=%wide.region_2.5_spmd.sunk | while | flops 1090649088 | bytes 31730348 | solution.py:109
  194.9 2.2 multiply_reduce_fusion.2
  198.6 2.1 fusion.79
  203.3 2.2 multiply_reduce_fusion.2
  211.7 2.2 multiply_reduce_fusion.2
  215.4 2.1 fusion.79
  220.1 2.2 multiply_reduce_fusion.2
  228.5 2.2 multiply_reduce_fusion.2
  236.9 2.2 multiply_reduce_fusion.2
  245.3 2.2 multiply_reduce_fusion.2
  253.7 2.3 multiply_reduce_fusion.2
  261.0 4.4 %all_to_all.25 = bf16[16,2,1,128,1,1,128]{6,3,0,5,4,2,1:T(8,128)(2,1)S(1)} all-to-all(bf16[16,2,1,128,1,1,128]{6,3,0,5,4,2,1:T(8,128)(2,1)S(1)} %copy.22), channel_id=1, replica_groups=mesh['groups'=2,'seq_0'=16,'seq_1'=2,'role'=4] {'seq_1'}, dimensions={1} | all-to-all | bytes 2097152 | tf_op jit(solution)/shard_map/all_to_all | solution.py:64
  266.4 10.9 %all-to-all-start.2 = ((bf16[16,2,1,128,1,1,128]{6,3,1,5,4,2,0:T(8,128)(2,1)}), bf16[16,2,1,128,1,1,128]{6,3,1,5,4,2,0:T(8,128)(2,1)}, u32[]{:S(2)}, u32[]{:S(2)}) async-start(bf16[16,2,1,128,1,1,128]{6,3,1,5,4,2,0:T(8,128)(2,1)} %copy.23), calls=%async_computation.2 | async-start | bytes 2097152 | tf_op jit(solution)/shard_map/all_to_all | solution.py:64
  288.9 9.5 %fusion.43 = bf16[1,2,160,384]{3,2,1,0:T(8,128)(2,1)} fusion(bf16[10368,384,1]{1,0,2:T(8,128)(2,1)} %bitcast.61, bf16[1,2,160,10368]{3,2,1,0:T(8,128)(2,1)} %slice_dynamic-update-slice_fusion, bf16[1,2,160,384]{3,2,1,0:T(8,128)(2,1)S(1)} %copy-done.6, f32[384]{0:T(512)S(1)} %copy-done.13), kind=kOutput, calls=%fused_computation.41 | convolution fusion | flops 2548531200 | bytes 15091200 | tf_op jit(solution)/shard_map/dot_general | solution.py:161
  298.4 24.3 %all-to-all-done.2 = bf16[16,2,1,128,1,1,128]{6,3,1,5,4,2,0:T(8,128)(2,1)} async-done(((bf16[16,2,1,128,1,1,128]{6,3,1,5,4,2,0:T(8,128)(2,1)}), bf16[16,2,1,128,1,1,128]{6,3,1,5,4,2,0:T(8,128)(2,1)}, u32[]{:S(2)}, u32[]{:S(2)}) %all-to-all-start.2) | async-done | bytes 1048608 | tf_op jit(solution)/shard_map/all_to_all | solution.py:64
  (120 shorter events, 70.2 us)
Async XLA Ops:
  0.6 4.5 %copy-start.8 = (bf16[1,128,4096]{2,1,0:T(8,128)(2,1)S(1)}, bf16[1,128,4096]{2,1,0:T(8,128)(2,1)}, u32[]{:S(2)}) copy-start(bf16[1,128,4096]{2,1,0:T(8,128)(2,1)} %param.14) | copy-start | bytes 3145732
  0.6 5.8 %copy-start.11 = (f32[4096]{0:T(1024)S(1)}, f32[4096]{0:T(1024)}, u32[]{:S(2)}) copy-start(f32[4096]{0:T(1024)} %param.15) | copy-start | bytes 49156
  0.7 6.5 %copy-start.12 = (f32[4096]{0:T(1024)S(1)}, f32[4096]{0:T(1024)}, u32[]{:S(2)}) copy-start(f32[4096]{0:T(1024)} %param.16) | copy-start | bytes 49156
  9.4 28.5 %copy-start.4 = (bf16[1,2,160,384]{3,2,1,0:T(8,128)(2,1)S(1)}, bf16[1,2,160,384]{3,2,1,0:T(8,128)(2,1)}, u32[]{:S(2)}) copy-start(bf16[1,2,160,384]{3,2,1,0:T(8,128)(2,1)} %param.17) | copy-start | bytes 737284
  9.4 28.6 %copy-start.10 = (f32[384]{0:T(512)S(1)}, f32[384]{0:T(512)}, u32[]{:S(2)}) copy-start(f32[384]{0:T(512)} %param.19) | copy-start | bytes 4612
  12.3 25.8 %copy-start.5 = (bf16[1,2,160,384]{3,2,1,0:T(8,128)(2,1)S(1)}, bf16[1,2,160,384]{3,2,1,0:T(8,128)(2,1)}, u32[]{:S(2)}) copy-start(bf16[1,2,160,384]{3,2,1,0:T(8,128)(2,1)} %param.17) | copy-start | bytes 737284
  12.3 33.4 %copy-start.7 = (bf16[2,2,160,384]{3,2,1,0:T(8,128)(2,1)S(1)}, bf16[2,2,160,384]{3,2,1,0:T(8,128)(2,1)}, u32[]{:S(2)}) copy-start(bf16[2,2,160,384]{3,2,1,0:T(8,128)(2,1)} %param.18) | copy-start | bytes 1474564
  12.3 176.5 %all-to-all-start = ((bf16[3,128,32,1,128]{4,1,0,3,2:T(8,128)(2,1)}), bf16[3,128,32,1,128]{4,1,0,3,2:T(8,128)(2,1)}, u32[]{:S(2)}, u32[]{:S(2)}) async-start(bf16[3,128,32,1,128]{4,1,0,3,2:T(8,128)(2,1)} %copy.21), calls=%async_computation | async-start | bytes 6291456 | tf_op jit(solution)/shard_map/all_to_all | solution.py:41
  38.3 9.6 %collective-permute-start = (bf16[1,2,160,384]{3,2,1,0:T(8,128)(2,1)S(1)}, bf16[1,2,160,384]{3,2,1,0:T(8,128)(2,1)S(1)}, u32[]{:S(2)}, u32[]{:S(2)}) collective-permute-start(bf16[1,2,160,384]{3,2,1,0:T(8,128)(2,1)S(1)} %fusion.61), channel_id=1, source_target_pairs={{0,2},{1,3},{4,6},{5,7},{8,10},{9,11},{12,14},{13,15},{16,18},{17,... | collective-permute-start | bytes 737288 | tf_op jit(solution)/shard_map/ppermute | solution.py:17
  43.3 9.9 %collective-permute-start.1 = (bf16[1,2,160,384]{3,2,1,0:T(8,128)(2,1)S(1)}, bf16[1,2,160,384]{3,2,1,0:T(8,128)(2,1)S(1)}, u32[]{:S(2)}, u32[]{:S(2)}) collective-permute-start(bf16[1,2,160,384]{3,2,1,0:T(8,128)(2,1)S(1)} %fusion.61), channel_id=1, source_target_pairs={{0,1},{1,2},{2,3},{4,5},{5,6},{6,7},{8,9},{9,10},{10,11},{12,13},{... | collective-permute-start | bytes 737288 | tf_op jit(solution)/shard_map/ppermute | solution.py:17
  53.4 123.3 %collective-permute-start.2 = (bf16[3,1,160,384]{3,2,1,0:T(8,128)(2,1)S(1)}, bf16[3,1,160,384]{3,2,1,0:T(8,128)(2,1)S(1)}, u32[]{:S(2)}, u32[]{:S(2)}) collective-permute-start(bf16[3,1,160,384]{3,2,1,0:T(8,128)(2,1)S(1)} %get-tuple-element.67), channel_id=1, source_target_pairs={{0,4},{4,8},{8,12},{12,16},{16,20},{20,24},{24,28},{28,32},{32,36}... | collective-permute-start | bytes 1105928 | tf_op jit(solution)/shard_map/ppermute | solution.py:25
  58.2 121.1 %collective-permute-start.3 = (bf16[3,1,160,384]{3,2,1,0:T(8,128)(2,1)S(1)}, bf16[3,1,160,384]{3,2,1,0:T(8,128)(2,1)S(1)}, u32[]{:S(2)}, u32[]{:S(2)}) collective-permute-start(bf16[3,1,160,384]{3,2,1,0:T(8,128)(2,1)S(1)} %get-tuple-element.68), channel_id=1, source_target_pairs={{4,0},{8,4},{12,8},{16,12},{20,16},{24,20},{28,24},{32,28},{36,32}... | collective-permute-start | bytes 1105928 | tf_op jit(solution)/shard_map/ppermute | solution.py:28
  176.7 12.1 %copy-start.2 = (bf16[3,1,160,384]{3,2,1,0:T(8,128)(2,1)}, bf16[3,1,160,384]{3,2,1,0:T(8,128)(2,1)S(1)}, u32[]{:S(2)}) copy-start(bf16[3,1,160,384]{3,2,1,0:T(8,128)(2,1)S(1)} %collective-permute-done.2) | copy-start | bytes 1105924
  179.2 9.6 %copy-start = (bf16[3,1,160,384]{3,2,1,0:T(8,128)(2,1)}, bf16[3,1,160,384]{3,2,1,0:T(8,128)(2,1)S(1)}, u32[]{:S(2)}) copy-start(bf16[3,1,160,384]{3,2,1,0:T(8,128)(2,1)S(1)} %collective-permute-done.3) | copy-start | bytes 1105924
  197.1 1.5 copy-start.9
  205.5 1.5 copy-start.9
  213.9 1.5 copy-start.9
  230.7 1.5 copy-start.9
  239.1 1.5 copy-start.9
  259.6 20.7 %copy-start.1 = (bf16[3,1,160,384]{3,2,1,0:T(8,128)(2,1)S(1)}, bf16[3,1,160,384]{3,2,1,0:T(8,128)(2,1)}, u32[]{:S(2)}) copy-start(bf16[3,1,160,384]{3,2,1,0:T(8,128)(2,1)} %copy-done) | copy-start | bytes 1105924
  259.6 23.0 %copy-start.3 = (bf16[3,1,160,384]{3,2,1,0:T(8,128)(2,1)S(1)}, bf16[3,1,160,384]{3,2,1,0:T(8,128)(2,1)}, u32[]{:S(2)}) copy-start(bf16[3,1,160,384]{3,2,1,0:T(8,128)(2,1)} %copy-done.2) | copy-start | bytes 1105924
  261.0 24.0 %copy-start.6 = (bf16[1,2,160,384]{3,2,1,0:T(8,128)(2,1)S(1)}, bf16[1,2,160,384]{3,2,1,0:T(8,128)(2,1)}, u32[]{:S(2)}) copy-start(bf16[1,2,160,384]{3,2,1,0:T(8,128)(2,1)} %param.17) | copy-start | bytes 737284
  265.3 23.6 %copy-start.13 = (f32[384]{0:T(512)S(1)}, f32[384]{0:T(512)}, u32[]{:S(2)}) copy-start(f32[384]{0:T(512)} %param.21) | copy-start | bytes 4612
  266.4 56.3 %all-to-all-start.2 = ((bf16[16,2,1,128,1,1,128]{6,3,1,5,4,2,0:T(8,128)(2,1)}), bf16[16,2,1,128,1,1,128]{6,3,1,5,4,2,0:T(8,128)(2,1)}, u32[]{:S(2)}, u32[]{:S(2)}) async-start(bf16[16,2,1,128,1,1,128]{6,3,1,5,4,2,0:T(8,128)(2,1)} %copy.23), calls=%async_computation.2 | async-start | bytes 2097152 | tf_op jit(solution)/shard_map/all_to_all | solution.py:64
  (3 other events, 4.5 us)
where the time goes:
time: 331 us; the launch traced here: 326 us
  waiting for transfers between devices  150 us (45%)
  starting transfers between devices  50.6 us (15%)
  matrix products  44.4 us (13%)
  local copies, waits for them, and re-layouts  37.2 us (11%)
  other arithmetic  23.1 us (7%)
  loops' own time  15 us (5%)
  blocking collectives  4.37 us (1%)
    ppermute x1, waiting for transfers between devices, extended(): lax.ppermute(lax.slice_in_dim(block, block.shape[dim] - width, None, axis...  117 us
    all_to_all x1, starting transfers between devices, sent_together(): lax.all_to_all(both, axis, split_axis=split_dim, concat_axis=concat_dim,...  25.6 us
    all_to_all x1, waiting for transfers between devices, exchange_in_order(): whole = lax.all_to_all(whole, axes[k], k, k, tiled=True)  24.3 us
    unnamed x48, local copies, waits for them, and re-layouts  19.2 us
    dot_general x8, matrix products, one_block(): jnp.einsum('qd,kd->qk', rows, k_head, preferred_element_type=jnp.float32)  18 us
    dot_general x8, matrix products, one_block(): jnp.dot(weights.astype(jnp.bfloat16), v_head, preferred_element_type=jnp....  17 us
    another operation x1, loops' own time, one_head(): return lax.map(one_block, starts).reshape(length, -1)  15 us
    reduce_sum x8, other arithmetic, one_block(): total = jnp.sum(weights, axis=1, keepdims=True)  12 us
  transfers between devices with their start and end apart: 6, of which 5 were waited for; matrix products, arithmetic and copies ran while one was open for 10% of the time, Pallas kernels for 0%

commit v1 on v0

v1 whole, which is shorter than its diff:
```python
import functools

import jax
import jax.numpy as jnp
from jax import lax
from jax.experimental import pallas as pl
from jax.experimental.pallas import tpu as pltpu
from jax.sharding import PartitionSpec as P

HEAD_DIM = 128
SEQ = "seq"
MESH = pl.DeviceIdType.MESH
LOG2_E = 1.4426950408889634


EPSILON = 1e-06


def from_behind(value, axis, steps):
    count = lax.axis_size(axis)
    leading, last = (max(0, -steps), min(count, count - steps))
    return lax.ppermute(value, axis, [(source, source + steps) for source in range(leading, last)])


def extended(block, axis, dim, width):
    count = lax.axis_size(axis)
    forward = [(i, i + 1) for i in range(count - 1)]
    backward = [(target, source) for source, target in forward]
    low = lax.ppermute(
        lax.slice_in_dim(block, block.shape[dim] - width, None, axis=dim), axis, forward
    )
    high = lax.ppermute(lax.slice_in_dim(block, 0, width, axis=dim), axis, backward)
    return jnp.concatenate([low, block, high], axis=dim)


def rms_scale(rows, gain):
    values_f = rows.astype(jnp.float32)
    mean_sq = jnp.mean(values_f * values_f, axis=-1, keepdims=True)
    return values_f * lax.rsqrt(mean_sq + EPSILON) * gain


def history(own, past, place):
    before = from_behind(own, "role", 1)
    earlier = from_behind(own, "role", 2)
    one_back = jnp.where(place >= 1, before, past[1:2])
    two_back = jnp.where(place >= 2, earlier, jnp.where(place >= 1, past[1:2], past[0:1]))
    return jnp.concatenate([two_back, one_back, own], axis=0)


def attention_kernel(
    count,
    q_in,
    k_in,
    v_in,
    q_gain,
    k_gain,
    out,
    q_raw,
    k_raw,
    v_raw,
    q_send,
    k_send,
    q_all,
    k_all,
    v_all,
    mixed,
    scores,
    load_sem,
    local_sem,
    send_sem,
    v_sem,
    k_sem,
    q_sem,
    o_sem,
    wave_sem,
):
    chips = count // 2
    half = chips // 2
    rows, width = q_raw.shape
    depth = width // count
    length = rows * count
    me = lax.axis_index(SEQ)
    chip, core = me // 2, me % 2

    def at(offset, other):
        return lax.rem(chip + offset + chips, chips) * 2 + lax.rem(core + other, 2)

    loads = [
        pltpu.make_async_copy(source, target, load_sem.at[i])
        for i, (source, target) in enumerate(((v_in, v_raw), (k_in, k_raw), (q_in, q_raw)))
    ]
    for load in loads:
        load.start()

    barrier = pltpu.get_barrier_semaphore()
    near = [at(0, 1), at(1, 0), at(1, 1), at(-1, 0), at(-1, 1)]
    for device in near:
        pl.semaphore_signal(barrier, inc=1, device_id={SEQ: device}, device_id_type=MESH)
    pl.semaphore_wait(barrier, len(near))

    def columns(head):
        return pl.ds(pl.multiple_of(head * depth, depth), depth)

    def to(device, source, target, sem, arrival):
        pltpu.make_async_remote_copy(
            src_ref=source,
            dst_ref=target,
            send_sem=sem,
            recv_sem=arrival,
            device_id={SEQ: device},
            device_id_type=MESH,
        ).start()

    def send_v(device):
        to(device, v_raw.at[:, columns(device)], v_all.at[me], send_sem.at[0], v_sem)

    def send_k(device):
        to(device, k_send.at[device], k_all.at[me], send_sem.at[1], k_sem)

    def send_q(device):
        to(device, q_send.at[device], q_all.at[me], send_sem.at[2], q_sem.at[me])

    loads[0].wait()
    own_v = pltpu.make_async_copy(v_raw.at[:, columns(me)], v_all.at[me], local_sem.at[0])
    own_v.start()
    send_v(at(0, 1))

    for d in range(1, half + 1):
        if d > 1:
            for device in near[1:]:
                pl.semaphore_signal(
                    wave_sem.at[d - 2], inc=1, device_id={SEQ: device}, device_id_type=MESH
                )
            pl.semaphore_wait(wave_sem.at[d - 2], len(near) - 1)
        for other in range(2):
            send_v(at(d, other))
            if d < half:
                send_v(at(-d, other))

    def normalize(raw, gain, target):
        step = 16

        def some(i, carry):
            at_rows = pl.ds(pl.multiple_of(i * step, step), step)
            wide = raw[at_rows, :].astype(jnp.float32)
            mean_sq = jnp.mean(wide * wide, axis=-1, keepdims=True)
            scaled = (wide * lax.rsqrt(mean_sq + EPSILON) * gain[...]).astype(jnp.bfloat16)
            for head in range(count):
                target[head, at_rows, :] = scaled[:, head * depth : (head + 1) * depth]
            return carry

        lax.fori_loop(0, rows // step, some, 0)

    def send_all(send):
        send(at(0, 1))

        def pair(d, carry):
            for other in range(2):
                send(at(d, other))
                send(at(-d, other))
            return carry

        lax.fori_loop(1, half, pair, 0)
        for other in range(2):
            send(at(half, other))

    loads[1].wait()
    normalize(k_raw, k_gain, k_send)
    own_k = pltpu.make_async_copy(k_send.at[me], k_all.at[me], local_sem.at[1])
    own_k.start()
    send_all(send_k)

    loads[2].wait()
    normalize(q_raw, q_gain, q_send)
    own_q = pltpu.make_async_copy(q_send.at[me], q_all.at[me], local_sem.at[2])
    own_q.start()
    send_all(send_q)

    def arrived(buffer, sem, blocks):
        pltpu.make_async_copy(buffer.at[pl.ds(0, blocks)], buffer.at[pl.ds(0, blocks)], sem).wait()

    own_v.wait()
    own_k.wait()
    own_q.wait()
    arrived(v_all, v_sem, count - 1)
    arrived(k_all, k_sem, count - 1)

    tile = 512
    blocks = tile // rows
    factor = LOG2_E * depth ** (-0.5)
    both = 2 * rows

    def attend(first):
        queries = q_all[pl.ds(first, 2)].reshape(both, depth)
        top = None
        for j in range(length // tile):
            keys = k_all[pl.ds(j * blocks, blocks)].reshape(tile, depth)
            part = lax.dot_general(
                queries, keys, (((1,), (1,)), ((), ())), preferred_element_type=jnp.float32
            )
            scores[:, pl.ds(j * tile, tile)] = part
            for g in range(tile // depth):
                piece = part[:, g * depth : (g + 1) * depth]
                top = piece if top is None else jnp.maximum(top, piece)
        top = jnp.max(top, axis=1, keepdims=True)
        total = jnp.zeros((both, depth), jnp.float32)
        result = jnp.zeros((both, depth), jnp.float32)
        for j in range(length // tile):
            weights = jnp.exp2((scores[:, pl.ds(j * tile, tile)] - top) * factor)
            for g in range(tile // depth):
                total = total + weights[:, g * depth : (g + 1) * depth]
            some_v = v_all[pl.ds(j * blocks, blocks)].reshape(tile, depth)
            result = result + jnp.dot(
                weights.astype(jnp.bfloat16), some_v, preferred_element_type=jnp.float32
            )
        result = result / jnp.sum(total, axis=1, keepdims=True)
        mixed[pl.ds(first, 2)] = result.astype(jnp.bfloat16).reshape(2, rows, depth)

    def send_o(device):
        to(device, mixed.at[device], out.at[me], send_sem.at[3], o_sem)

    def q_arrived(device):
        pltpu.make_async_copy(q_all.at[device], q_all.at[device], q_sem.at[device]).wait()

    q_arrived(at(0, 1))
    attend(chip * 2)
    own_o = pltpu.make_async_copy(mixed.at[me], out.at[me], local_sem.at[3])
    own_o.start()
    send_o(at(0, 1))

    def chip_step(k, carry):
        offset = (k + 1) // 2 * (2 * (k % 2) - 1)
        first = at(offset, 0) // 2 * 2
        q_arrived(first)
        q_arrived(first + 1)
        attend(first)
        send_o(first)
        send_o(first + 1)
        return carry

    lax.fori_loop(1, chips, chip_step, 0)

    own_o.wait()
    arrived(out, o_sem, count - 1)
    arrived(v_all, send_sem.at[0], count - 1)
    arrived(k_all, send_sem.at[1], count - 1)
    arrived(q_all, send_sem.at[2], count - 1)
    arrived(mixed, send_sem.at[3], count - 1)


def attention(queries, keys, values, q_gain, k_gain):
    count = lax.axis_size(SEQ)
    rows, width = queries.shape
    depth = width // count
    blocks = (count, rows, depth)
    anywhere = pl.BlockSpec(memory_space=pl.ANY)
    in_vmem = pl.BlockSpec(memory_space=pltpu.VMEM)
    low = jnp.bfloat16
    return pl.pallas_call(
        functools.partial(attention_kernel, count),
        out_shape=jax.ShapeDtypeStruct(blocks, low),
        in_specs=[anywhere, anywhere, anywhere, in_vmem, in_vmem],
        out_specs=anywhere,
        scratch_shapes=[
            pltpu.VMEM((rows, width), low),
            pltpu.VMEM((rows, width), low),
            pltpu.VMEM((rows, width), low),
            pltpu.VMEM(blocks, low),
            pltpu.VMEM(blocks, low),
            pltpu.VMEM(blocks, low),
            pltpu.VMEM(blocks, low),
            pltpu.VMEM(blocks, low),
            pltpu.VMEM(blocks, low),
            pltpu.VMEM((2 * rows, rows * count), jnp.float32),
            pltpu.SemaphoreType.DMA((3,)),
            pltpu.SemaphoreType.DMA((4,)),
            pltpu.SemaphoreType.DMA((4,)),
            pltpu.SemaphoreType.DMA,
            pltpu.SemaphoreType.DMA,
            pltpu.SemaphoreType.DMA((count,)),
            pltpu.SemaphoreType.DMA,
            pltpu.SemaphoreType.REGULAR((count // 4 - 1,)),
        ],
        compiler_params=pltpu.CompilerParams(
            collective_id=0, has_side_effects=True, vmem_limit_bytes=40 * 1024 * 1024
        ),
        cost_estimate=pl.CostEstimate(
            flops=4 * (rows * count) ** 2 * depth,
            bytes_accessed=8 * rows * width,
            transcendentals=(rows * count) ** 2,
        ),
    )(queries, keys, values, q_gain.reshape(1, width), k_gain.reshape(1, width))


def body(
    queries,
    keys,
    values,
    q_gain,
    k_gain,
    latent_frames,
    frame_cache,
    vae_gain,
    conv_weight,
    conv_bias,
):
    tok_local = queries.shape[1]
    width = queries.shape[2]
    activated_own = jax.nn.silu(rms_scale(latent_frames, vae_gain)).astype(jnp.bfloat16)
    activated_past = jax.nn.silu(rms_scale(frame_cache, vae_gain)).astype(jnp.bfloat16)
    place = lax.axis_index("role")
    stacked = history(activated_own, activated_past, place)
    stacked = extended(stacked, SEQ, 1, 1)
    stacked = jnp.pad(stacked, ((0, 0), (0, 0), (1, 1), (0, 0)))
    rows = latent_frames.shape[1]
    cols = latent_frames.shape[2]
    chans = latent_frames.shape[3]
    pieces = []
    for a in range(3):
        for b in range(3):
            for e in range(3):
                pieces.append(stacked[a, b : b + rows, e : e + cols, :])
    columns = jnp.concatenate(pieces, axis=-1).reshape(rows * cols, 27 * chans)
    weight = conv_weight.reshape(27 * chans, chans)
    conv = jnp.dot(columns, weight, preferred_element_type=jnp.float32).reshape(
        1, rows, cols, chans
    )
    decoded = (latent_frames.astype(jnp.float32) + conv + conv_bias).astype(jnp.bfloat16)
    blocks = attention(queries[0], keys[0], values[0], q_gain, k_gain)
    attended = jnp.moveaxis(blocks, 0, 1).reshape(1, tok_local, width)
    return (attended, decoded)


def solution(mesh):
    in_specs = (
        P(("groups", "role"), SEQ, None),
        P(("groups", "role"), SEQ, None),
        P(("groups", "role"), SEQ, None),
        P(),
        P(),
        P(("groups", "role"), SEQ, None, None),
        P("groups", SEQ, None, None),
        P(),
        P(),
        P(),
    )
    out_specs = (P(("groups", "role"), SEQ, None), P(("groups", "role"), SEQ, None, None))
    return jax.shard_map(body, mesh=mesh, in_specs=in_specs, out_specs=out_specs, check_vma=False)
```

time: 331 us -> 249 us (0.75)
  Pallas kernels: 0 us -> 194 us
  waiting for transfers between devices: 150 us -> 0.65 us
  matrix products: 44.4 us -> 4.32 us
  local copies, waits for them, and re-layouts: 37.2 us -> 5.41 us
  starting transfers between devices: 50.6 us -> 28.7 us
  loops' own time: 15 us -> 0 us
  other arithmetic: 23.1 us -> 13.2 us
  blocking collectives: 4.37 us -> 0 us
    pallas_call x0 -> x1, Pallas kernels: none -> 194 us  [attention(): pl.pallas_call(functools.partial(attention_kernel, count), out_shape=jax....]
    ppermute x1, waiting for transfers between devices: 117 us -> 0.01 us  [extended(): lax.ppermute(lax.slice_in_dim(block, block.shape[dim] - width, None, axis...]
    all_to_all x2 -> x0, starting transfers between devices: 36.5 us -> none  [the longest x1 25.6 us: sent_together(): lax.all_to_all(both, axis, split_axis=split_dim, concat_axis=concat_dim,...]
    dot_general x16 -> x0, matrix products: 35 us -> none  [the longest x8 18 us: one_block(): jnp.einsum('qd,kd->qk', rows, k_head, preferred_element_type=jnp.float32)]
    all_to_all x2 -> x0, waiting for transfers between devices: 24.3 us -> none  [the longest x1 24.3 us: exchange_in_order(): whole = lax.all_to_all(whole, axes[k], k, k, tiled=True)]
    unnamed x48, local copies, waits for them, and re-layouts: 19.2 us -> 3.68 us
    another operation x1 -> x0, loops' own time: 15 us -> none  [one_head(): return lax.map(one_block, starts).reshape(length, -1)]
    reduce_sum x8 -> x0, other arithmetic: 12 us -> none  [one_block(): total = jnp.sum(weights, axis=1, keepdims=True)]
  transfers between devices with their start and end apart: 6 -> 4, of which waited for: 5 -> 1; matrix products, arithmetic and copies ran while one was open for 10% -> 2% of each run, Pallas kernels for 0% -> 78%
where the time goes in v1:
time: 249 us; the launch traced here: 247 us
  Pallas kernels  194 us (78%)
  starting transfers between devices  28.7 us (12%)
  other arithmetic  13.2 us (5%)
  local copies, waits for them, and re-layouts  5.41 us (2%)
  matrix products  4.32 us (2%)
    pallas_call x1, Pallas kernels, attention(): pl.pallas_call(functools.partial(attention_kernel, count), out_shape=jax....  194 us
    ppermute x1, starting transfers between devices, extended(): lax.ppermute(lax.slice_in_dim(block, 0, width, axis=dim), axis, backward)  10.5 us
    ppermute x1, starting transfers between devices, extended(): lax.ppermute(lax.slice_in_dim(block, block.shape[dim] - width, None, axis...  10 us
    ppermute x2, starting transfers between devices, from_behind(): lax.ppermute(value, axis, [(source, source + steps) for source in range(l...  8.18 us
    unnamed x8, other arithmetic  6.25 us
  transfers between devices with their start and end apart: 4, of which 1 were waited for; matrix products, arithmetic and copies ran while one was open for 2% of the time, Pallas kernels for 78%

profile of v1, /device:TPU:33, one launch (start us, length us, event | category | flops | bytes accessed | tf_op | source)
XLA Modules:
  0.0 246.9 jit_solution(9399398437845343602)
XLA Ops:
  0.7 1.2 fusion.28
  1.9 1.2 fusion.35
  3.1 5.8 %collective-permute-start = (bf16[1,2,160,384]{3,2,1,0:T(8,128)(2,1)S(1)}, bf16[1,2,160,384]{3,2,1,0:T(8,128)(2,1)S(1)}, u32[]{:S(2)}, u32[]{:S(2)}) collective-permute-start(bf16[1,2,160,384]{3,2,1,0:T(8,128)(2,1)S(1)} %fusion.35), channel_id=1, source_target_pairs={{0,2},{1,3},{4,6},{5,7},{8,10},{9,11},{12,14},{13,15},{16,18},{17,... | collective-permute-start | bytes 737288 | tf_op jit(solution)/shard_map/ppermute | solution.py:22
  8.9 2.4 collective-permute-start.1
  11.3 1.3 fusion.20
  12.6 1.4 fusion.27
  14.0 0.6 collective-permute-done.1
  14.7 0.1 pad_maximum_fusion
  14.8 1.0 fusion.39
  15.8 10.0 %collective-permute-start.2 = (bf16[3,1,160,384]{3,2,1,0:T(8,128)(2,1)}, bf16[3,1,160,384]{3,2,1,0:T(8,128)(2,1)}, u32[]{:S(2)}, u32[]{:S(2)}) collective-permute-start(bf16[3,1,160,384]{3,2,1,0:T(8,128)(2,1)} %get-tuple-element.4), channel_id=1, source_target_pairs={{0,4},{4,8},{8,12},{12,16},{16,20},{20,24},{24,28},{28,32},{32,36}... | collective-permute-start | bytes 1105928 | tf_op jit(solution)/shard_map/ppermute | solution.py:29
  25.8 10.5 %collective-permute-start.3 = (bf16[3,1,160,384]{3,2,1,0:T(8,128)(2,1)}, bf16[3,1,160,384]{3,2,1,0:T(8,128)(2,1)}, u32[]{:S(2)}, u32[]{:S(2)}) collective-permute-start(bf16[3,1,160,384]{3,2,1,0:T(8,128)(2,1)} %get-tuple-element.5), channel_id=1, source_target_pairs={{4,0},{8,4},{12,8},{16,12},{20,16},{24,20},{28,24},{32,28},{36,32}... | collective-permute-start | bytes 1105928 | tf_op jit(solution)/shard_map/ppermute | solution.py:32
  36.4 1.2 copy-done.2
  37.6 193.6 %shard_map.113 = bf16[32,128,128]{2,1,0:T(8,128)(2,1)S(1)} custom-call(bf16[128,4096]{1,0:T(8,128)(2,1)S(1)} %bitcast.31, bf16[128,4096]{1,0:T(8,128)(2,1)S(1)} %bitcast.32, bf16[128,4096]{1,0:T(8,128)(2,1)S(1)} %bitcast.33, f32[1,4096]{1,0:T(1,128)S(1)} %bitcast.34, f32[1,4096]{1,0:T(1,128)S(1)} %bitcast.35), custom_call_target="tpu_custom_call" | custom-call | flops 8589934592 | bytes 4194304 | tf_op jit(solution)/shard_map/pallas_call | solution.py:259
  231.3 0.7 copy.12
  231.9 1.3 copy.13
  233.2 1.7 select_maximum_fusion
  235.0 0.9 maximum_dynamic-update-slice_fusion.3
  236.3 1.1 maximum_dynamic-update-slice_fusion.2
  237.5 1.0 maximum_dynamic-update-slice_fusion.1
  238.8 1.1 maximum_dynamic-update-slice_fusion
  240.0 0.9 fusion.37
  241.1 0.3 constant_dynamic-update-slice_fusion
  241.5 0.9 fusion.36
  242.6 4.3 %fusion.17 = bf16[1,2,160,384]{3,2,1,0:T(8,128)(2,1)} fusion(bf16[10368,384,1]{1,0,2:T(8,128)(2,1)S(1)} %bitcast.39, bf16[1,2,160,10368]{3,2,1,0:T(8,128)(2,1)S(1)} %slice_dynamic-update-slice_fusion, bf16[1,2,160,384]{3,2,1,0:T(8,128)(2,1)S(1)} %copy-done.9, f32[384]{0:T(512)S(1)} %copy-done.11), kind=kOutput, calls=%fused_computation.17 | convolution fusion | flops 2548531200 | bytes 15091200 | tf_op jit(solution)/shard_map/dot_general | solution.py:325
  (54 shorter events, 1.3 us)
Async XLA Ops:
  0.6 35.7 %copy-start = (bf16[1,128,4096]{2,1,0:T(8,128)(2,1)S(1)}, bf16[1,128,4096]{2,1,0:T(8,128)(2,1)}, u32[]{:S(2)}) copy-start(bf16[1,128,4096]{2,1,0:T(8,128)(2,1)} %param.10) | copy-start | bytes 3145732
  0.6 35.7 %copy-start.1 = (bf16[1,128,4096]{2,1,0:T(8,128)(2,1)S(1)}, bf16[1,128,4096]{2,1,0:T(8,128)(2,1)}, u32[]{:S(2)}) copy-start(bf16[1,128,4096]{2,1,0:T(8,128)(2,1)} %param.11) | copy-start | bytes 3145732
  0.7 35.7 %copy-start.3 = (f32[4096]{0:T(1024)S(1)}, f32[4096]{0:T(1024)}, u32[]{:S(2)}) copy-start(f32[4096]{0:T(1024)} %param.13) | copy-start | bytes 49156
  0.7 35.7 %copy-start.4 = (f32[4096]{0:T(1024)S(1)}, f32[4096]{0:T(1024)}, u32[]{:S(2)}) copy-start(f32[4096]{0:T(1024)} %param.14) | copy-start | bytes 49156
  3.1 33.2 %copy-start.7 = (bf16[1,2,160,384]{3,2,1,0:T(8,128)(2,1)}, bf16[1,2,160,384]{3,2,1,0:T(8,128)(2,1)S(1)}, u32[]{:S(2)}) copy-start(bf16[1,2,160,384]{3,2,1,0:T(8,128)(2,1)S(1)} %fusion.35) | copy-start | bytes 737284
  3.1 10.9 %collective-permute-start = (bf16[1,2,160,384]{3,2,1,0:T(8,128)(2,1)S(1)}, bf16[1,2,160,384]{3,2,1,0:T(8,128)(2,1)S(1)}, u32[]{:S(2)}, u32[]{:S(2)}) collective-permute-start(bf16[1,2,160,384]{3,2,1,0:T(8,128)(2,1)S(1)} %fusion.35), channel_id=1, source_target_pairs={{0,2},{1,3},{4,6},{5,7},{8,10},{9,11},{12,14},{13,15},{16,18},{17,... | collective-permute-start | bytes 737288 | tf_op jit(solution)/shard_map/ppermute | solution.py:22
  8.9 5.7 %collective-permute-start.1 = (bf16[1,2,160,384]{3,2,1,0:T(8,128)(2,1)S(1)}, bf16[1,2,160,384]{3,2,1,0:T(8,128)(2,1)S(1)}, u32[]{:S(2)}, u32[]{:S(2)}) collective-permute-start(bf16[1,2,160,384]{3,2,1,0:T(8,128)(2,1)S(1)} %fusion.35), channel_id=1, source_target_pairs={{0,1},{1,2},{2,3},{4,5},{5,6},{6,7},{8,9},{9,10},{10,11},{12,13},{... | collective-permute-start | bytes 737288 | tf_op jit(solution)/shard_map/ppermute | solution.py:22
  14.7 21.6 %copy-start.5 = (bf16[1,2,160,384]{3,2,1,0:T(8,128)(2,1)}, bf16[1,2,160,384]{3,2,1,0:T(8,128)(2,1)S(1)}, u32[]{:S(2)}) copy-start(bf16[1,2,160,384]{3,2,1,0:T(8,128)(2,1)S(1)} %get-tuple-element.7) | copy-start | bytes 737284
  15.8 217.4 %collective-permute-start.2 = (bf16[3,1,160,384]{3,2,1,0:T(8,128)(2,1)}, bf16[3,1,160,384]{3,2,1,0:T(8,128)(2,1)}, u32[]{:S(2)}, u32[]{:S(2)}) collective-permute-start(bf16[3,1,160,384]{3,2,1,0:T(8,128)(2,1)} %get-tuple-element.4), channel_id=1, source_target_pairs={{0,4},{4,8},{8,12},{12,16},{16,20},{20,24},{24,28},{28,32},{32,36}... | collective-permute-start | bytes 1105928 | tf_op jit(solution)/shard_map/ppermute | solution.py:29
  25.8 207.4 %collective-permute-start.3 = (bf16[3,1,160,384]{3,2,1,0:T(8,128)(2,1)}, bf16[3,1,160,384]{3,2,1,0:T(8,128)(2,1)}, u32[]{:S(2)}, u32[]{:S(2)}) collective-permute-start(bf16[3,1,160,384]{3,2,1,0:T(8,128)(2,1)} %get-tuple-element.5), channel_id=1, source_target_pairs={{4,0},{8,4},{12,8},{16,12},{20,16},{24,20},{28,24},{32,28},{36,32}... | collective-permute-start | bytes 1105928 | tf_op jit(solution)/shard_map/ppermute | solution.py:32
  36.4 1.2 copy-start.2
  231.2 3.7 %copy-start.6 = (bf16[1,2,160,384]{3,2,1,0:T(8,128)(2,1)S(1)}, bf16[1,2,160,384]{3,2,1,0:T(8,128)(2,1)}, u32[]{:S(2)}) copy-start(bf16[1,2,160,384]{3,2,1,0:T(8,128)(2,1)} %copy-done.5) | copy-start | bytes 737284
  231.2 3.7 %copy-start.8 = (bf16[1,2,160,384]{3,2,1,0:T(8,128)(2,1)S(1)}, bf16[1,2,160,384]{3,2,1,0:T(8,128)(2,1)}, u32[]{:S(2)}) copy-start(bf16[1,2,160,384]{3,2,1,0:T(8,128)(2,1)} %copy-done.7) | copy-start | bytes 737284
  235.9 5.2 %copy-start.9 = (bf16[1,2,160,384]{3,2,1,0:T(8,128)(2,1)S(1)}, bf16[1,2,160,384]{3,2,1,0:T(8,128)(2,1)}, u32[]{:S(2)}) copy-start(bf16[1,2,160,384]{3,2,1,0:T(8,128)(2,1)} %param.15) | copy-start | bytes 737284
  235.9 5.2 %copy-start.10 = (f32[384]{0:T(512)S(1)}, f32[384]{0:T(512)}, u32[]{:S(2)}) copy-start(f32[384]{0:T(512)} %param.17) | copy-start | bytes 4612
  236.2 6.3 %slice-start = ((s8[7962624]{0:T(1024)(128)(4,1)}), s8[4194304]{0:T(1024)(128)(4,1)S(1)}, s32[]{:S(2)}) async-start(s8[7962624]{0:T(1024)(128)(4,1)} %bitcast.37), calls=%async_computation | async-start | bytes 8388608
  237.4 5.2 %copy-start.11 = (f32[384]{0:T(512)S(1)}, f32[384]{0:T(512)}, u32[]{:S(2)}) copy-start(f32[384]{0:T(512)} %param.19) | copy-start | bytes 4612
  238.8 3.8 %slice-start.1 = ((s8[7962624]{0:T(1024)(128)(4,1)}), s8[3768320]{0:T(1024)(128)(4,1)S(1)}, s32[]{:S(2)}) async-start(s8[7962624]{0:T(1024)(128)(4,1)} %bitcast.37), calls=%async_computation.1 | async-start | bytes 7536640

commit v2 on v1

v2 whole, which is shorter than its diff:
```python
import functools

import jax
import jax.numpy as jnp
from jax import lax
from jax.experimental import pallas as pl
from jax.experimental.pallas import tpu as pltpu
from jax.sharding import PartitionSpec as P

HEAD_DIM = 128
SEQ = "seq"
ROLE = "role"
MESH = pl.DeviceIdType.MESH
VMEM_BYTES = 67043328
LOG2_E = 1.4426950408889634


EPSILON = 1e-06


def block_kernel(
    count,
    roles,
    q_in,
    k_in,
    v_in,
    q_gain_in,
    k_gain_in,
    latent_in,
    cache_in,
    vae_gain_in,
    weight_in,
    bias_in,
    out,
    decoded_out,
    q_raw,
    k_raw,
    v_raw,
    q_gain,
    k_gain,
    latent,
    cache,
    vae_gain,
    weight,
    bias,
    frames,
    past,
    past_halo,
    sums,
    decoded,
    q_send,
    k_send,
    q_all,
    k_all,
    v_all,
    mixed,
    scores,
    load_sem,
    local_sem,
    send_sem,
    v_sem,
    k_sem,
    q_sem,
    o_sem,
    wave_sem,
    halo_send,
    halo_sem,
    frame_send,
    frame_sem,
    piece_send,
    piece_sem,
):
    chips = count // 2
    half = chips // 2
    rows, width = q_raw.shape
    depth = width // count
    length = rows * count
    me = lax.axis_index(SEQ)
    chip, core = me // 2, me % 2
    role = lax.axis_index(ROLE)
    image_rows, cols, chans = latent.shape
    pasts = cache.shape[0]
    shares = roles // pasts
    share = cols // shares
    last = image_rows + 1

    def at(offset, other):
        return lax.rem(chip + offset + chips, chips) * 2 + lax.rem(core + other, 2)

    loads = [
        pltpu.make_async_copy(source, target, load_sem.at[i])
        for i, (source, target) in enumerate(
            (
                (v_in, v_raw),
                (latent_in, latent),
                (cache_in, cache),
                (vae_gain_in, vae_gain),
                (k_in, k_raw),
                (k_gain_in, k_gain),
                (q_in, q_raw),
                (q_gain_in, q_gain),
                (weight_in, weight),
                (bias_in, bias),
            )
        )
    ]
    v_load, latent_load, cache_load, vae_gain_load = loads[:4]
    k_load, k_gain_load, q_load, q_gain_load, weight_load, bias_load = loads[4:]
    for load in loads:
        load.start()

    barrier = pltpu.get_barrier_semaphore()
    near = [at(0, 1), at(1, 0), at(1, 1), at(-1, 0), at(-1, 1)]
    for device in near:
        pl.semaphore_signal(barrier, inc=1, device_id={SEQ: device}, device_id_type=MESH)
    for step in range(1, roles):
        pl.semaphore_signal(
            barrier,
            inc=1,
            device_id={ROLE: lax.rem(role + step, roles)},
            device_id_type=MESH,
        )
    pl.semaphore_wait(barrier, len(near) + roles - 1)

    def columns(head):
        return pl.ds(pl.multiple_of(head * depth, depth), depth)

    def to(device, source, target, sem, arrival):
        pltpu.make_async_remote_copy(
            src_ref=source,
            dst_ref=target,
            send_sem=sem,
            recv_sem=arrival,
            device_id={SEQ: device},
            device_id_type=MESH,
        ).start()

    def send_v(device):
        to(device, v_raw.at[:, columns(device)], v_all.at[me], send_sem.at[0], v_sem)

    def send_k(device):
        to(device, k_send.at[device], k_all.at[me], send_sem.at[1], k_sem)

    def send_q(device):
        to(device, q_send.at[device], q_all.at[me], send_sem.at[2], q_sem.at[me])

    v_load.wait()
    own_v = pltpu.make_async_copy(v_raw.at[:, columns(me)], v_all.at[me], local_sem.at[0])
    own_v.start()
    send_v(at(0, 1))

    def activated(values):
        wide = values.astype(jnp.float32)
        mean_sq = jnp.mean(wide * wide, axis=-1, keepdims=True)
        scaled = wide * lax.rsqrt(mean_sq + EPSILON) * vae_gain[...].reshape(1, chans)
        return (scaled * lax.logistic(scaled)).astype(jnp.bfloat16)

    def activate():
        latent_load.wait()
        cache_load.wait()
        vae_gain_load.wait()
        for row in range(image_rows):
            frames[2, 1 + row] = activated(latent[row])
            for frame in range(pasts):
                past[frame, row] = activated(cache[frame, row])

        @pl.when(me == 0)
        def _():
            frames[2, 0] = jnp.zeros((cols, chans), frames.dtype)
            past_halo[0] = jnp.zeros((share, chans), past_halo.dtype)

        @pl.when(me == count - 1)
        def _():
            frames[2, last] = jnp.zeros((cols, chans), frames.dtype)
            past_halo[1] = jnp.zeros((share, chans), past_halo.dtype)

    my_past = role // shares
    my_cols = pl.ds(pl.multiple_of(lax.rem(role, shares) * share, share), share)

    def halo_copies(device, side):
        edge = 0 if side == 0 else image_rows - 1
        landing = 1 - side
        pairs = (
            (frames.at[2, 1 + edge], frames.at[2, landing * last]),
            (past.at[my_past, edge, my_cols], past_halo.at[landing]),
        )
        return [
            pltpu.make_async_remote_copy(
                src_ref=source,
                dst_ref=target,
                send_sem=halo_send.at[side, i],
                recv_sem=halo_sem.at[landing, i],
                device_id={SEQ: device},
                device_id_type=MESH,
            )
            for i, (source, target) in enumerate(pairs)
        ]

    def each_side(act):
        @pl.when(me > 0)
        def _():
            act(me - 1, 0)

        @pl.when(me < count - 1)
        def _():
            act(me + 1, 1)

    def send_halos():
        def start(device, side):
            for copy in halo_copies(device, side):
                copy.start()

        each_side(start)

    def wait_halos():
        def wait(device, side):
            for i, target in enumerate((frames.at[2, side * last], past_halo.at[side])):
                pltpu.make_async_copy(target, target, halo_sem.at[side, i]).wait()

        each_side(wait)

    def frame_copy(ahead):
        return pltpu.make_async_remote_copy(
            src_ref=frames.at[2],
            dst_ref=frames.at[2 - ahead],
            send_sem=frame_send.at[ahead - 1],
            recv_sem=frame_sem.at[ahead - 1],
            device_id={ROLE: role + ahead},
            device_id_type=MESH,
        )

    def piece_place(frame, target, side, source_role):
        part = pl.ds(pl.multiple_of(lax.rem(source_role, shares) * share, share), share)
        return frames.at[frame - target, side * last, part]

    def pieces(act_remote, act_local):
        for target in range(pasts):
            for frame in range(target, pasts):
                for side in range(2):
                    mine = jnp.logical_and(my_past == frame, role != target)
                    here = jnp.logical_and(my_past == frame, role == target)

                    @pl.when(mine)
                    def _():
                        act_remote(frame, target, side)

                    @pl.when(here)
                    def _():
                        act_local(frame, target, side)

    def piece_copy(frame, target, side):
        return pltpu.make_async_remote_copy(
            src_ref=past_halo.at[side],
            dst_ref=piece_place(frame, target, side, role),
            send_sem=piece_send.at[target, side],
            recv_sem=piece_sem.at[role, side],
            device_id={ROLE: target},
            device_id_type=MESH,
        )

    def own_piece(frame, target, side):
        return pltpu.make_async_copy(
            past_halo.at[side],
            piece_place(frame, target, side, role),
            piece_send.at[target, side],
        )

    def pass_on():
        for ahead in (1, 2):

            @pl.when(role + ahead < roles)
            def _():
                frame_copy(ahead).start()

        pieces(
            lambda *which: piece_copy(*which).start(), lambda *which: own_piece(*which).start()
        )
        for target in range(pasts):

            @pl.when(role == target)
            def _():
                for frame in range(target, pasts):
                    frames[frame - target, 1 : 1 + image_rows] = past[frame]

    def wait_frames():
        for ahead in (1, 2):

            @pl.when(role >= ahead)
            def _():
                target = frames.at[2 - ahead]
                pltpu.make_async_copy(target, target, frame_sem.at[ahead - 1]).wait()

        for target in range(pasts):

            @pl.when(role == target)
            def _():
                for source_role in range(target * shares, roles):
                    if source_role == target:
                        continue
                    for side in range(2):
                        place = piece_place(source_role // shares, target, side, source_role)
                        pltpu.make_async_copy(place, place, piece_sem.at[source_role, side]).wait()

        pieces(lambda *which: None, lambda *which: own_piece(*which).wait())

    def wait_conv_sends():
        def wait(device, side):
            for copy in halo_copies(device, side):
                copy.wait_send()

        each_side(wait)
        for ahead in (1, 2):

            @pl.when(role + ahead < roles)
            def _():
                frame_copy(ahead).wait_send()

        pieces(lambda *which: piece_copy(*which).wait_send(), lambda *which: None)

    def convolve():
        flat = image_rows * cols
        sums[...] = jnp.zeros_like(sums)

        def tap(i, carry):
            a, b = i // 3, i % 3
            window = frames[a, pl.ds(b, image_rows)].reshape(flat, chans)
            for e in range(3):
                sums[e] += jnp.dot(window, weight[a, b, e], preferred_element_type=jnp.float32)
            return carry

        lax.fori_loop(0, 9, tap, 0)
        index = lax.broadcasted_iota(jnp.int32, (cols, chans), 0)
        for row in range(image_rows):
            part = pl.ds(row * cols, cols)
            left = jnp.where(index == 0, 0.0, pltpu.roll(sums[0, part], 1, 0))
            right = jnp.where(index == cols - 1, 0.0, pltpu.roll(sums[2, part], cols - 1, 0))
            conv = sums[1, part] + left + right
            decoded[row] = (latent[row].astype(jnp.float32) + conv + bias[...].reshape(1, chans)).astype(
                decoded.dtype
            )

    for d in range(1, half + 1):
        if d > 1:
            for device in near[1:]:
                pl.semaphore_signal(
                    wave_sem.at[d - 2], inc=1, device_id={SEQ: device}, device_id_type=MESH
                )
            pl.semaphore_wait(wave_sem.at[d - 2], len(near) - 1)
        for other in range(2):
            send_v(at(d, other))
            if d < half:
                send_v(at(-d, other))
        if d == 2:
            activate()
            send_halos()

    def normalize(raw, gain, target):
        step = 16

        def some(i, carry):
            at_rows = pl.ds(pl.multiple_of(i * step, step), step)
            wide = raw[at_rows, :].astype(jnp.float32)
            mean_sq = jnp.mean(wide * wide, axis=-1, keepdims=True)
            scaled = (wide * lax.rsqrt(mean_sq + EPSILON) * gain[...]).astype(jnp.bfloat16)
            for head in range(count):
                target[head, at_rows, :] = scaled[:, head * depth : (head + 1) * depth]
            return carry

        lax.fori_loop(0, rows // step, some, 0)

    def send_all(send):
        send(at(0, 1))

        def pair(d, carry):
            for other in range(2):
                send(at(d, other))
                send(at(-d, other))
            return carry

        lax.fori_loop(1, half, pair, 0)
        for other in range(2):
            send(at(half, other))

    k_load.wait()
    k_gain_load.wait()
    normalize(k_raw, k_gain, k_send)
    own_k = pltpu.make_async_copy(k_send.at[me], k_all.at[me], local_sem.at[1])
    own_k.start()
    send_all(send_k)

    q_load.wait()
    q_gain_load.wait()
    normalize(q_raw, q_gain, q_send)
    own_q = pltpu.make_async_copy(q_send.at[me], q_all.at[me], local_sem.at[2])
    own_q.start()

    def farthest_first(i, carry):
        d = half - i
        for other in range(2):
            send_q(at(d, other))
            send_q(at(-d, other))
        return carry

    for other in range(2):
        send_q(at(half, other))
    lax.fori_loop(1, half, farthest_first, 0)
    send_q(at(0, 1))

    wait_halos()
    pass_on()
    weight_load.wait()
    bias_load.wait()
    wait_frames()
    convolve()
    decoded_store = pltpu.make_async_copy(decoded, decoded_out, local_sem.at[4])
    decoded_store.start()

    def arrived(buffer, sem, blocks):
        pltpu.make_async_copy(buffer.at[pl.ds(0, blocks)], buffer.at[pl.ds(0, blocks)], sem).wait()

    own_v.wait()
    own_k.wait()
    own_q.wait()
    arrived(v_all, v_sem, count - 1)
    arrived(k_all, k_sem, count - 1)

    tile = 512
    blocks = tile // rows
    factor = LOG2_E * depth ** (-0.5)
    both = 2 * rows

    def attend(first):
        queries = q_all[pl.ds(first, 2)].reshape(both, depth)
        top = None
        for j in range(length // tile):
            keys = k_all[pl.ds(j * blocks, blocks)].reshape(tile, depth)
            part = lax.dot_general(
                queries, keys, (((1,), (1,)), ((), ())), preferred_element_type=jnp.float32
            )
            scores[:, pl.ds(j * tile, tile)] = part
            for g in range(tile // depth):
                piece = part[:, g * depth : (g + 1) * depth]
                top = piece if top is None else jnp.maximum(top, piece)
        top = jnp.max(top, axis=1, keepdims=True)
        total = jnp.zeros((both, depth), jnp.float32)
        result = jnp.zeros((both, depth), jnp.float32)
        for j in range(length // tile):
            weights = jnp.exp2((scores[:, pl.ds(j * tile, tile)] - top) * factor)
            for g in range(tile // depth):
                total = total + weights[:, g * depth : (g + 1) * depth]
            some_v = v_all[pl.ds(j * blocks, blocks)].reshape(tile, depth)
            result = result + jnp.dot(
                weights.astype(jnp.bfloat16), some_v, preferred_element_type=jnp.float32
            )
        result = result / jnp.sum(total, axis=1, keepdims=True)
        mixed[pl.ds(first, 2)] = result.astype(jnp.bfloat16).reshape(2, rows, depth)

    def send_o(device):
        to(device, mixed.at[device], out.at[:, columns(me)], send_sem.at[3], o_sem)

    def q_arrived(device):
        pltpu.make_async_copy(q_all.at[device], q_all.at[device], q_sem.at[device]).wait()

    q_arrived(at(0, 1))
    attend(chip * 2)
    own_o = pltpu.make_async_copy(mixed.at[me], out.at[:, columns(me)], local_sem.at[3])
    own_o.start()
    send_o(at(0, 1))

    def chip_step(k, carry):
        j = chips - k
        offset = (j + 1) // 2 * (2 * (j % 2) - 1)
        first = at(offset, 0) // 2 * 2
        q_arrived(first)
        q_arrived(first + 1)
        attend(first)
        send_o(first)
        send_o(first + 1)
        return carry

    lax.fori_loop(1, chips, chip_step, 0)

    wait_conv_sends()
    decoded_store.wait()
    own_o.wait()
    arrived(mixed, o_sem, count - 1)
    arrived(v_all, send_sem.at[0], count - 1)
    arrived(k_all, send_sem.at[1], count - 1)
    arrived(q_all, send_sem.at[2], count - 1)
    arrived(mixed, send_sem.at[3], count - 1)


def store_kernel(attended, decoded, attended_out, decoded_out, wide, image, load_sem, store_sem):
    pieces = load_sem.shape[0] - 1
    step = wide.shape[0] // pieces
    moves = [(decoded, image, decoded_out)]
    for i in range(pieces):
        part = pl.ds(i * step, step)
        moves.append((attended.at[part], wide.at[part], attended_out.at[part]))
    loads = [pltpu.make_async_copy(m[0], m[1], load_sem.at[i]) for i, m in enumerate(moves)]
    stores = [pltpu.make_async_copy(m[1], m[2], store_sem.at[i]) for i, m in enumerate(moves)]
    for load in loads:
        load.start()
    for load, store in zip(loads, stores):
        load.wait()
        store.start()
    for store in stores:
        store.wait()


def body(
    queries,
    keys,
    values,
    q_gain,
    k_gain,
    latent_frames,
    frame_cache,
    vae_gain,
    conv_weight,
    conv_bias,
):
    count, roles = lax.axis_size(SEQ), lax.axis_size(ROLE)
    _, rows, width = queries.shape
    depth = HEAD_DIM
    pasts = frame_cache.shape[0]
    _, image_rows, cols, chans = latent_frames.shape
    blocks = (count, rows, depth)
    in_hbm = pl.BlockSpec(memory_space=pltpu.HBM)
    anywhere = pl.BlockSpec(memory_space=pl.ANY)
    low, wide = jnp.bfloat16, jnp.float32
    dma = pltpu.SemaphoreType.DMA
    attended, decoded = pl.pallas_call(
        functools.partial(block_kernel, count, roles),
        out_shape=(
            jax.ShapeDtypeStruct((rows, width), low),
            jax.ShapeDtypeStruct((image_rows, cols, chans), low),
        ),
        in_specs=[in_hbm] * 10,
        out_specs=(anywhere, anywhere),
        scratch_shapes=[
            pltpu.VMEM((rows, width), low),
            pltpu.VMEM((rows, width), low),
            pltpu.VMEM((rows, width), low),
            pltpu.VMEM((1, width), wide),
            pltpu.VMEM((1, width), wide),
            pltpu.VMEM((image_rows, cols, chans), low),
            pltpu.VMEM((pasts, image_rows, cols, chans), low),
            pltpu.VMEM((chans,), wide),
            pltpu.VMEM(conv_weight.shape, low),
            pltpu.VMEM((chans,), wide),
            pltpu.VMEM((3, image_rows + 2, cols, chans), low),
            pltpu.VMEM((pasts, image_rows, cols, chans), low),
            pltpu.VMEM((2, cols * pasts // roles, chans), low),
            pltpu.VMEM((3, image_rows * cols, chans), wide),
            pltpu.VMEM((image_rows, cols, chans), low),
            pltpu.VMEM(blocks, low),
            pltpu.VMEM(blocks, low),
            pltpu.VMEM(blocks, low),
            pltpu.VMEM(blocks, low),
            pltpu.VMEM(blocks, low),
            pltpu.VMEM(blocks, low),
            pltpu.VMEM((2 * rows, rows * count), wide),
            dma((10,)),
            dma((5,)),
            dma((4,)),
            dma,
            dma,
            dma((count,)),
            dma,
            pltpu.SemaphoreType.REGULAR((count // 4 - 1,)),
            dma((2, 2)),
            dma((2, 2)),
            dma((2,)),
            dma((2,)),
            dma((pasts, 2)),
            dma((roles, 2)),
        ],
        compiler_params=pltpu.CompilerParams(
            collective_id=0, has_side_effects=True, vmem_limit_bytes=VMEM_BYTES
        ),
    )(
        queries[0],
        keys[0],
        values[0],
        q_gain.reshape(1, width),
        k_gain.reshape(1, width),
        latent_frames[0],
        frame_cache,
        vae_gain,
        conv_weight,
        conv_bias,
    )
    attended, decoded = pl.pallas_call(
        store_kernel,
        out_shape=(
            jax.ShapeDtypeStruct((rows, width), low),
            jax.ShapeDtypeStruct((image_rows, cols, chans), low),
        ),
        in_specs=[anywhere] * 2,
        out_specs=(anywhere, anywhere),
        scratch_shapes=[
            pltpu.VMEM((rows, width), low),
            pltpu.VMEM((image_rows, cols, chans), low),
            dma((5,)),
            dma((5,)),
        ],
        compiler_params=pltpu.CompilerParams(vmem_limit_bytes=VMEM_BYTES),
    )(attended, decoded)
    return attended[None], decoded[None]


def solution(mesh):
    in_specs = (
        P(("groups", "role"), SEQ, None),
        P(("groups", "role"), SEQ, None),
        P(("groups", "role"), SEQ, None),
        P(),
        P(),
        P(("groups", "role"), SEQ, None, None),
        P("groups", SEQ, None, None),
        P(),
        P(),
        P(),
    )
    out_specs = (P(("groups", "role"), SEQ, None), P(("groups", "role"), SEQ, None, None))
    return jax.shard_map(body, mesh=mesh, in_specs=in_specs, out_specs=out_specs, check_vma=False)
```

time: 249 us -> 213 us (0.86)
  starting transfers between devices: 28.7 us -> 0 us
  Pallas kernels: 194 us -> 212 us
  other arithmetic: 13.2 us -> 0 us
  local copies, waits for them, and re-layouts: 5.41 us -> 0 us
  matrix products: 4.32 us -> 0 us
    ppermute x4 -> x0, starting transfers between devices: 28.7 us -> none  [the longest x1 10.5 us: extended(): lax.ppermute(lax.slice_in_dim(block, 0, width, axis=dim), axis, backward)]
    pallas_call x1 -> x2, Pallas kernels: 194 us -> 212 us  [the longest x1 210 us: body(): pl.pallas_call(functools.partial(block_kernel, count, roles), out_shape=(...]
    unnamed x8 -> x0, other arithmetic: 6.25 us -> none
    dot_general x1 -> x0, matrix products: 4.32 us -> none  [body(): jnp.dot(columns, weight, preferred_element_type=jnp.float32)]
    unnamed x48 -> x0, local copies, waits for them, and re-layouts: 3.68 us -> none
    convert_element_type x2 -> x0, other arithmetic: 2.57 us -> none  [the longest x1 1.4 us: body(): jax.nn.silu(rms_scale(frame_cache, vae_gain)).astype(jnp.bfloat16)]
  transfers between devices with their start and end apart: 4 -> 0, of which waited for: 1 -> 0; matrix products, arithmetic and copies ran while one was open for 2% -> 0% of each run, Pallas kernels for 78% -> 0%
where the time goes in v2:
time: 213 us
  Pallas kernels  212 us (100%)
    pallas_call x1, Pallas kernels, body(): pl.pallas_call(functools.partial(block_kernel, count, roles), out_shape=(...  210 us

profile of v2, /device:TPU:33, one launch (start us, length us, event | category | flops | bytes accessed | tf_op | source)
XLA Modules:
  0.0 212.6 jit_solution(10533368698073929021)
XLA Ops:
  0.6 209.8 %shard_map.113 = (bf16[128,4096]{1,0:T(8,128)(2,1)}, bf16[2,160,384]{2,1,0:T(8,128)(2,1)}) custom-call(bf16[128,4096]{1,0:T(8,128)(2,1)} %bitcast.8, bf16[128,4096]{1,0:T(8,128)(2,1)} %bitcast.9, bf16[128,4096]{1,0:T(8,128)(2,1)} %bitcast.10, f32[1,4096]{1,0:T(1,128)} %bitcast.12, f32[1,4096]{1,0:T(1,128)} %bitcast.13, bf16[2,160,384]{2,1,0:T(8,128)(2,1)} %bitcast.11, ...), custom_call_target="tpu_custom_call" | custom-call | tf_op jit(solution)/shard_map/pallas_call | solution.py:533
  210.5 2.1 %shard_map.114 = (bf16[128,4096]{1,0:T(8,128)(2,1)}, bf16[2,160,384]{2,1,0:T(8,128)(2,1)}) custom-call(bf16[128,4096]{1,0:T(8,128)(2,1)} %get-tuple-element.6.attended, bf16[2,160,384]{2,1,0:T(8,128)(2,1)} %get-tuple-element.7.decoded), custom_call_target="tpu_custom_call" | custom-call | tf_op jit(solution)/shard_map/pallas_call | solution.py:594

commit v3 on v2

--- a/solution.py
+++ b/solution.py
@@ -106,8 +106,7 @@
     ]
     v_load, latent_load, cache_load, vae_gain_load = loads[:4]
     k_load, k_gain_load, q_load, q_gain_load, weight_load, bias_load = loads[4:]
-    for load in loads:
-        load.start()
+    v_load.start()
 
     barrier = pltpu.get_barrier_semaphore()
     near = [at(0, 1), at(1, 0), at(1, 1), at(-1, 0), at(-1, 1)]
@@ -148,6 +147,8 @@
     own_v = pltpu.make_async_copy(v_raw.at[:, columns(me)], v_all.at[me], local_sem.at[0])
     own_v.start()
     send_v(at(0, 1))
+    for load in loads[1:-2]:
+        load.start()
 
     def activated(values):
         wide = values.astype(jnp.float32)
@@ -350,7 +351,9 @@
             send_v(at(d, other))
             if d < half:
                 send_v(at(-d, other))
-        if d == 2:
+        if d == half // 2:
+            weight_load.start()
+            bias_load.start()
             activate()
             send_halos()
 

time: 213 us -> 213 us (level)
  no operation moved by 1% of the time
where the time goes in v3:
time: 213 us
  Pallas kernels  212 us (100%)
    pallas_call x1, Pallas kernels, body(): pl.pallas_call(functools.partial(block_kernel, count, roles), out_shape=(...  210 us

profile of v3, /device:TPU:33, one launch (start us, length us, event | category | flops | bytes accessed | tf_op | source)
XLA Modules:
  0.0 212.6 jit_solution(955705979871171875)
XLA Ops:
  0.6 209.8 %shard_map.113 = (bf16[128,4096]{1,0:T(8,128)(2,1)}, bf16[2,160,384]{2,1,0:T(8,128)(2,1)}) custom-call(bf16[128,4096]{1,0:T(8,128)(2,1)} %bitcast.8, bf16[128,4096]{1,0:T(8,128)(2,1)} %bitcast.9, bf16[128,4096]{1,0:T(8,128)(2,1)} %bitcast.10, f32[1,4096]{1,0:T(1,128)} %bitcast.12, f32[1,4096]{1,0:T(1,128)} %bitcast.13, bf16[2,160,384]{2,1,0:T(8,128)(2,1)} %bitcast.11, ...), custom_call_target="tpu_custom_call" | custom-call | tf_op jit(solution)/shard_map/pallas_call | solution.py:536
  210.5 2.1 %shard_map.114 = (bf16[128,4096]{1,0:T(8,128)(2,1)}, bf16[2,160,384]{2,1,0:T(8,128)(2,1)}) custom-call(bf16[128,4096]{1,0:T(8,128)(2,1)} %get-tuple-element.6.attended, bf16[2,160,384]{2,1,0:T(8,128)(2,1)} %get-tuple-element.7.decoded), custom_call_target="tpu_custom_call" | custom-call | tf_op jit(solution)/shard_map/pallas_call | solution.py:597

commit v4 on v2

--- a/solution.py
+++ b/solution.py
@@ -461,12 +461,6 @@
     def q_arrived(device):
         pltpu.make_async_copy(q_all.at[device], q_all.at[device], q_sem.at[device]).wait()
 
-    q_arrived(at(0, 1))
-    attend(chip * 2)
-    own_o = pltpu.make_async_copy(mixed.at[me], out.at[:, columns(me)], local_sem.at[3])
-    own_o.start()
-    send_o(at(0, 1))
-
     def chip_step(k, carry):
         j = chips - k
         offset = (j + 1) // 2 * (2 * (j % 2) - 1)
@@ -479,6 +473,11 @@
         return carry
 
     lax.fori_loop(1, chips, chip_step, 0)
+    q_arrived(at(0, 1))
+    attend(chip * 2)
+    own_o = pltpu.make_async_copy(mixed.at[me], out.at[:, columns(me)], local_sem.at[3])
+    own_o.start()
+    send_o(at(0, 1))
 
     wait_conv_sends()
     decoded_store.wait()

time: 213 us -> 213 us (level)
  no operation moved by 1% of the time
where the time goes in v4:
time: 213 us
  Pallas kernels  212 us (100%)
    pallas_call x1, Pallas kernels, body(): pl.pallas_call(functools.partial(block_kernel, count, roles), out_shape=(...  210 us

profile of v4, /device:TPU:33, one launch (start us, length us, event | category | flops | bytes accessed | tf_op | source)
XLA Modules:
  0.0 212.6 jit_solution(2752434527231711330)
XLA Ops:
  0.6 209.8 %shard_map.113 = (bf16[128,4096]{1,0:T(8,128)(2,1)}, bf16[2,160,384]{2,1,0:T(8,128)(2,1)}) custom-call(bf16[128,4096]{1,0:T(8,128)(2,1)} %bitcast.8, bf16[128,4096]{1,0:T(8,128)(2,1)} %bitcast.9, bf16[128,4096]{1,0:T(8,128)(2,1)} %bitcast.10, f32[1,4096]{1,0:T(1,128)} %bitcast.12, f32[1,4096]{1,0:T(1,128)} %bitcast.13, bf16[2,160,384]{2,1,0:T(8,128)(2,1)} %bitcast.11, ...), custom_call_target="tpu_custom_call" | custom-call | tf_op jit(solution)/shard_map/pallas_call | solution.py:532
  210.5 2.1 %shard_map.114 = (bf16[128,4096]{1,0:T(8,128)(2,1)}, bf16[2,160,384]{2,1,0:T(8,128)(2,1)}) custom-call(bf16[128,4096]{1,0:T(8,128)(2,1)} %get-tuple-element.6.attended, bf16[2,160,384]{2,1,0:T(8,128)(2,1)} %get-tuple-element.7.decoded), custom_call_target="tpu_custom_call" | custom-call | tf_op jit(solution)/shard_map/pallas_call | solution.py:593
